TPU v7x, 16 devices: a 4x2x1 block of a 4x4x8 slice. The times are simulated.
16 devices in a mesh: dp: 2 (over y, z), fsdp: 8 (over x, core).
Axes of the slice: x: 4, y: 2, z: 1, core: 2. Of those that a mesh axis runs over, the one named last changes fastest.
The devices are a block of a 4x4x8 slice.
Arguments:
- hidden: bfloat16 [16, 64, 2048], P(('dp', 'fsdp')), parts along dimension 0
- attn_norm: bfloat16 [2, 2048], P(None, 'fsdp')
- w_q: bfloat16 [2, 2048, 32, 64], P(None, 'fsdp')
- w_k: bfloat16 [2, 2048, 8, 64], P(None, 'fsdp')
- w_v: bfloat16 [2, 2048, 8, 64], P(None, 'fsdp')
- w_o: bfloat16 [2, 2048, 2048], P(None, 'fsdp')
- mlp_norm: bfloat16 [2, 2048], P(None, 'fsdp')
- w_gate: bfloat16 [2, 2048, 8192], P(None, 'fsdp')
- w_up: bfloat16 [2, 2048, 8192], P(None, 'fsdp')
- w_down: bfloat16 [2, 8192, 2048], P(None, 'fsdp')
Outputs:
- output: bfloat16 [16, 64, 2048], P(('dp', 'fsdp')), parts along dimension 0
There are 2 independent parts. A program takes and returns all parts, laid end to end along the dimension named above; an argument that names none is the same for every part.
All inputs are finite; a program needn't handle non-finite values.
Results may differ from a plain program's by a relative error of at most 0.02.
Values are sent between devices in bfloat16 or wider.
A program may use at most 768 MiB of HBM per device.

v0:
```python
import jax
import jax.numpy as jnp
from jax import lax
from jax.sharding import PartitionSpec as P

ROPE_THETA = 500000.0
NORM_EPS = 1e-5


def rms_norm(hidden, gain):
    wide_hidden = hidden.astype(jnp.float32)
    inv_rms = lax.rsqrt(jnp.mean(wide_hidden * wide_hidden, axis=-1, keepdims=True) + NORM_EPS)
    return (wide_hidden * inv_rms * gain.astype(jnp.float32)).astype(jnp.bfloat16)


def rope_tables(seq_len, head_dim):
    half = head_dim // 2
    inv_freq = jnp.power(ROPE_THETA, -(jnp.arange(half, dtype=jnp.float32) * 2.0 / head_dim))
    angles = jnp.arange(seq_len, dtype=jnp.float32)[:, None] * inv_freq[None, :]
    return jnp.cos(angles)[:, None, :], jnp.sin(angles)[:, None, :]


def apply_rope(proj, cos_table, sin_table):
    half = proj.shape[-1] // 2
    first = proj[..., :half]
    second = proj[..., half:]
    rotated = jnp.concatenate([first * cos_table - second * sin_table, second * cos_table + first * sin_table], axis=-1)
    return rotated.astype(jnp.bfloat16)


def decoder_layer(hidden, attn_gain, w_q, w_k, w_v, w_o, mlp_gain, w_gate, w_up, w_down):
    batch, seq_len = hidden.shape[0], hidden.shape[1]
    heads, head_dim = w_q.shape[1], w_q.shape[2]
    kv_heads = w_k.shape[1]
    group = heads // kv_heads
    cos_table, sin_table = rope_tables(seq_len, head_dim)
    normed = rms_norm(hidden, attn_gain)
    queries = apply_rope(jnp.einsum("bsd,dhe->bshe", normed, w_q, preferred_element_type=jnp.float32), cos_table, sin_table)
    keys_rot = apply_rope(jnp.einsum("bsd,dhe->bshe", normed, w_k, preferred_element_type=jnp.float32), cos_table, sin_table)
    values = jnp.einsum("bsd,dhe->bshe", normed, w_v, preferred_element_type=jnp.float32).astype(jnp.bfloat16)
    q_grouped = queries.reshape(batch, seq_len, kv_heads, group, head_dim)
    scores = jnp.einsum("bqkgd,bskd->bkgqs", q_grouped, keys_rot, preferred_element_type=jnp.float32) * head_dim ** -0.5
    row_pos = lax.broadcasted_iota(jnp.int32, (seq_len, seq_len), 0)
    col_pos = lax.broadcasted_iota(jnp.int32, (seq_len, seq_len), 1)
    probs = jax.nn.softmax(jnp.where(row_pos >= col_pos, scores, -jnp.inf), axis=-1).astype(jnp.bfloat16)
    attended = jnp.einsum("bkgqs,bskd->bqkgd", probs, values, preferred_element_type=jnp.float32).astype(jnp.bfloat16)
    attended = attended.reshape(batch, seq_len, heads * head_dim)
    after_attn = (hidden.astype(jnp.float32) + jnp.einsum("bsf,fd->bsd", attended, w_o, preferred_element_type=jnp.float32)).astype(jnp.bfloat16)
    mlp_in = rms_norm(after_attn, mlp_gain)
    gate_proj = jnp.einsum("bsd,df->bsf", mlp_in, w_gate, preferred_element_type=jnp.float32).astype(jnp.bfloat16)
    up_proj = jnp.einsum("bsd,df->bsf", mlp_in, w_up, preferred_element_type=jnp.float32).astype(jnp.bfloat16)
    gated = (jax.nn.silu(gate_proj.astype(jnp.float32)) * up_proj.astype(jnp.float32)).astype(jnp.bfloat16)
    return (after_attn.astype(jnp.float32) + jnp.einsum("bsf,fd->bsd", gated, w_down, preferred_element_type=jnp.float32)).astype(jnp.bfloat16)


def solution(mesh):
    batch_spec = P(("dp", "fsdp"), None, None)
    gain_spec = P(None, "fsdp")
    proj_spec = P(None, "fsdp", None, None)
    mat_spec = P(None, "fsdp", None)

    def local_forward(hidden, attn_norm, w_q, w_k, w_v, w_o, mlp_norm, w_gate, w_up, w_down):
        for layer in range(w_q.shape[0]):
            whole = [lax.all_gather(shard[layer], "fsdp", axis=0, tiled=True) for shard in (attn_norm, w_q, w_k, w_v, w_o, mlp_norm, w_gate, w_up, w_down)]
            hidden = decoder_layer(hidden, whole[0], whole[1], whole[2], whole[3], whole[4], whole[5], whole[6], whole[7], whole[8])
        return hidden

    return jax.shard_map(local_forward, mesh=mesh, in_specs=(batch_spec, gain_spec, proj_spec, proj_spec, proj_spec, mat_spec, gain_spec, mat_spec, mat_spec, mat_spec), out_specs=batch_spec, check_vma=False)
```

profile of v0, /device:TPU:113, one launch (start us, length us, event | category | flops | bytes accessed | tf_op | source)
XLA Modules:
  0.0 1269.1 jit_solution(6581706133829382046)
XLA Ops:
  6.6 2.0 fusion.188
  8.6 0.1 all-gather.33.cloned.1.call-start
  8.7 1.9 fusion.187
  10.7 0.1 all-gather.37.cloned.1.call-start
  10.8 3.1 fusion.186
  13.9 0.1 all-gather.39.cloned.1.call-start
  14.0 1.5 fusion.185
  15.6 0.1 all-gather.41.cloned.1.call-start
  15.6 5.9 fusion.182
  21.6 0.1 all-gather.43.cloned.1.call-start
  21.7 5.9 fusion.183
  27.7 0.1 all-gather.45.cloned.1.call-start
  27.7 6.1 fusion.184
  33.9 0.1 all-gather.51.cloned.1.call-start
  33.9 0.7 all-gather.51.cloned.1.call-update
  34.8 0.7 all-gather.49.cloned.1.call-update
  35.5 0.6 all-gather.47.cloned.1.call-update
  36.2 0.7 all-gather.53.cloned.1.call-update
  37.0 0.6 all-gather.55.cloned.1.call-update
  37.7 0.7 all-gather.57.cloned.1.call-update
  38.4 0.1 all-gather.59.cloned.1.call-start
  38.4 0.6 all-gather.59.cloned.1.call-update
  39.0 19.3 %all-gather = bf16[1,2048]{1,0:T(2,128)(2,1)S(1)} all-gather(bf16[1,256]{1,0:T(2,128)(2,1)S(1)} %get-tuple-element.30), channel_id=2, replica_groups=mesh['dp'=2,'fsdp'=8] {'fsdp'}, dimensions={1}, use_global_device_ids=true | all-gather | bytes 4608 | tf_op jit(solution)/shard_map/all_gather | solution.py:64
  58.4 22.6 %all-gather.5 = bf16[1,2048]{1,0:T(2,128)(2,1)S(1)} all-gather(bf16[1,256]{1,0:T(2,128)(2,1)S(1)} %get-tuple-element.28), channel_id=7, replica_groups=mesh['dp'=2,'fsdp'=8] {'fsdp'}, dimensions={1}, use_global_device_ids=true | all-gather | bytes 4608 | tf_op jit(solution)/shard_map/all_gather | solution.py:64
  81.0 21.6 %all-gather.9 = bf16[1,2048]{1,0:T(2,128)(2,1)S(1)} all-gather(bf16[1,256]{1,0:T(2,128)(2,1)S(1)} %get-tuple-element.29), channel_id=11, replica_groups=mesh['dp'=2,'fsdp'=8] {'fsdp'}, dimensions={1}, use_global_device_ids=true | all-gather | bytes 4608 | tf_op jit(solution)/shard_map/all_gather | solution.py:64
  102.6 20.9 %all-gather.14 = bf16[1,2048]{1,0:T(2,128)(2,1)S(1)} all-gather(bf16[1,256]{1,0:T(2,128)(2,1)S(1)} %get-tuple-element.27), channel_id=16, replica_groups=mesh['dp'=2,'fsdp'=8] {'fsdp'}, dimensions={1}, use_global_device_ids=true | all-gather | bytes 4608 | tf_op jit(solution)/shard_map/all_gather | solution.py:64
  123.6 0.2 fusion.125
  123.8 0.1 fusion.171
  123.9 2.4 fusion.178
  126.4 2.4 fusion.180
  128.8 5.8 fusion.176
  134.6 0.1 subtract_convert_fusion.1
  134.8 0.3 copy.11
  135.1 0.3 copy.12
  135.3 0.7 fusion.191
  136.0 0.2 fusion.123
  136.3 0.3 convolution_convert_fusion.1
  136.6 22.4 %all-gather.39.cloned.1.call-done = bf16[1,2048,2048]{2,1,0:T(8,128)(2,1)} async-done(((bf16[1,256,2048]{2,1,0:T(8,128)(2,1)}), bf16[1,2048,2048]{2,1,0:T(8,128)(2,1)}) %all-gather.39.cloned.1.call-update) | async-done | bytes 8388624 | tf_op jit(solution)/shard_map/all_gather | solution.py:64
  159.0 5.1 multiply_reduce_fusion.2
  164.1 149.3 %all-gather.41.cloned.1.call-done = bf16[1,2048,8192]{2,1,0:T(8,128)(2,1)} async-done(((bf16[1,256,8192]{2,1,0:T(8,128)(2,1)}), bf16[1,2048,8192]{2,1,0:T(8,128)(2,1)}) %all-gather.41.cloned.1.call-update) | async-done | bytes 33554448 | tf_op jit(solution)/shard_map/all_gather | solution.py:64
  313.4 13.6 %fusion.15 = f32[64,8192]{1,0:T(8,128)S(1)} fusion(bf16[1,2048,8192]{2,1,0:T(8,128)(2,1)} %all-gather.41.cloned.1.call-done, f32[1,64,2048]{2,1,0:T(8,128)S(1)} %get-tuple-element.36, f32[2048]{0:T(1024)S(1)} %bitcast.279, f32[64]{0:T(128)S(1)} %add_rsqrt_fusion.2), kind=kOutput, calls=%fused_computation.13 | convolution fusion | flops 2148925440 | bytes 36184320 | tf_op jit(solution)/shard_map/bsd,df->bsf/dot_general | solution.py:50
  327.0 141.4 %all-gather.43.cloned.1.call-done = bf16[1,2048,8192]{2,1,0:T(8,128)(2,1)} async-done(((bf16[1,256,8192]{2,1,0:T(8,128)(2,1)}), bf16[1,2048,8192]{2,1,0:T(8,128)(2,1)}) %all-gather.43.cloned.1.call-update) | async-done | bytes 33554448 | tf_op jit(solution)/shard_map/all_gather | solution.py:64
  468.4 155.2 %all-gather.45.cloned.1.call-done = bf16[1,8192,2048]{2,1,0:T(8,128)(2,1)} async-done(((bf16[1,1024,2048]{2,1,0:T(8,128)(2,1)}), bf16[1,8192,2048]{2,1,0:T(8,128)(2,1)}) %all-gather.45.cloned.1.call-update) | async-done | bytes 33554448 | tf_op jit(solution)/shard_map/all_gather | solution.py:64
  623.7 24.8 %multiply_reduce_fusion.1 = (f32[64]{0:T(128)S(1)}, f32[1,64,2048]{2,1,0:T(8,128)S(1)}) fusion(f32[1,64,2048]{2,1,0:T(8,128)S(1)} %get-tuple-element.36, bf16[1,8192,2048]{2,1,0:T(8,128)(2,1)} %all-gather.45.cloned.1.call-done, bf16[1,2048,8192]{2,1,0:T(8,128)(2,1)} %all-gather.43.cloned.1.call-done, f32[64,8192]{1,0:T(8,128)S(1)} %fusion.15, ...), kind=kOutput, calls=%fused_computation.87 | convolution fusion | flops 4300210176 | bytes 70263296 | tf_op jit(solution)/shard_map/bsf,fd->bsd/dot_general | solution.py:53
  648.5 0.1 fusion.140
  648.6 26.3 %all-gather.51.cloned.1.call-done = bf16[1,2048,32,64]{1,3,2,0:T(8,128)(2,1)} async-done(((bf16[1,256,32,64]{1,3,2,0:T(8,128)(2,1)}), bf16[1,2048,32,64]{1,3,2,0:T(8,128)(2,1)}) %all-gather.51.cloned.1.call-update) | async-done | bytes 8388624 | tf_op jit(solution)/shard_map/all_gather | solution.py:64
  675.0 5.7 fusion.199
  680.7 0.1 subtract_convert_fusion
  680.8 0.3 copy.15
  681.1 0.3 copy.16
  681.4 18.4 %all-gather.49.cloned.1.call-done = bf16[1,2048,8,64]{1,3,2,0:T(8,128)(2,1)} async-done(((bf16[1,256,8,64]{1,3,2,0:T(8,128)(2,1)}), bf16[1,2048,8,64]{1,3,2,0:T(8,128)(2,1)}) %all-gather.49.cloned.1.call-update) | async-done | bytes 2097168 | tf_op jit(solution)/shard_map/all_gather | solution.py:64
  699.8 2.3 fusion.198
  702.2 0.7 fusion.196
  702.9 0.2 fusion.124
  703.1 21.4 %all-gather.47.cloned.1.call-done = bf16[1,2048,8,64]{1,3,2,0:T(8,128)(2,1)} async-done(((bf16[1,256,8,64]{1,3,2,0:T(8,128)(2,1)}), bf16[1,2048,8,64]{1,3,2,0:T(8,128)(2,1)}) %all-gather.47.cloned.1.call-update) | async-done | bytes 2097168 | tf_op jit(solution)/shard_map/all_gather | solution.py:64
  724.5 2.3 fusion.197
  726.8 0.3 convolution_convert_fusion
  727.1 45.4 %all-gather.53.cloned.1.call-done = bf16[1,2048,2048]{2,1,0:T(8,128)(2,1)} async-done(((bf16[1,256,2048]{2,1,0:T(8,128)(2,1)}), bf16[1,2048,2048]{2,1,0:T(8,128)(2,1)}) %all-gather.53.cloned.1.call-update) | async-done | bytes 8388624 | tf_op jit(solution)/shard_map/all_gather | solution.py:64
  772.5 5.1 multiply_reduce_fusion
  777.6 149.3 %all-gather.55.cloned.1.call-done = bf16[1,2048,8192]{2,1,0:T(8,128)(2,1)} async-done(((bf16[1,256,8192]{2,1,0:T(8,128)(2,1)}), bf16[1,2048,8192]{2,1,0:T(8,128)(2,1)}) %all-gather.55.cloned.1.call-update) | async-done | bytes 33554448 | tf_op jit(solution)/shard_map/all_gather | solution.py:64
  926.9 13.6 %fusion.33 = f32[64,8192]{1,0:T(8,128)S(1)} fusion(bf16[1,2048,8192]{2,1,0:T(8,128)(2,1)} %all-gather.55.cloned.1.call-done, f32[1,64,2048]{2,1,0:T(8,128)S(1)} %get-tuple-element.42, f32[2048]{0:T(1024)S(1)} %bitcast.277, f32[64]{0:T(128)S(1)} %add_rsqrt_fusion), kind=kOutput, calls=%fused_computation.19 | convolution fusion | flops 2148925440 | bytes 36184320 | tf_op jit(solution)/shard_map/bsd,df->bsf/dot_general | solution.py:50
  940.5 141.6 %all-gather.57.cloned.1.call-done = bf16[1,2048,8192]{2,1,0:T(8,128)(2,1)} async-done(((bf16[1,256,8192]{2,1,0:T(8,128)(2,1)}), bf16[1,2048,8192]{2,1,0:T(8,128)(2,1)}) %all-gather.57.cloned.1.call-update) | async-done | bytes 33554448 | tf_op jit(solution)/shard_map/all_gather | solution.py:64
  1082.1 155.1 %all-gather.59.cloned.1.call-done = bf16[1,8192,2048]{2,1,0:T(8,128)(2,1)} async-done(((bf16[1,1024,2048]{2,1,0:T(8,128)(2,1)}), bf16[1,8192,2048]{2,1,0:T(8,128)(2,1)}) %all-gather.59.cloned.1.call-update) | async-done | bytes 33554448 | tf_op jit(solution)/shard_map/all_gather | solution.py:64
  1237.2 25.4 %fusion.90 = bf16[1,64,2048]{2,1,0:T(8,128)(2,1)} fusion(f32[1,64,2048]{2,1,0:T(8,128)S(1)} %get-tuple-element.42, bf16[1,8192,2048]{2,1,0:T(8,128)(2,1)} %all-gather.59.cloned.1.call-done, bf16[1,2048,8192]{2,1,0:T(8,128)(2,1)} %all-gather.57.cloned.1.call-done, f32[64,8192]{1,0:T(8,128)S(1)} %fusion.33, f32[2048]{0:T(1024)S(1)} %bitcast.278, ...), kind=kOutput, calls=%fused_computation.38 | convolution fusion | flops 4299816960 | bytes 70000896 | tf_op jit(solution)/shard_map/bsf,fd->bsd/dot_general | solution.py:53
  (38 shorter events, 1.0 us)
Async XLA Ops:
  6.5 7.5 copy-start.1
  6.5 117.4 %all-gather.35.cloned.1.call-start = ((), (), s32[]{:S(2)}) async-start(), calls=%async_computation.1 | async-start | bytes 2359296 | tf_op jit(solution)/shard_map/all_gather | solution.py:64
  8.6 117.8 %all-gather.33.cloned.1.call-start = ((), (), s32[]{:S(2)}) async-start(), calls=%async_computation | async-start | bytes 2359296 | tf_op jit(solution)/shard_map/all_gather | solution.py:64
  10.7 118.1 %all-gather.37.cloned.1.call-start = ((), (), s32[]{:S(2)}) async-start(), calls=%async_computation.2 | async-start | bytes 9437184 | tf_op jit(solution)/shard_map/all_gather | solution.py:64
  13.9 145.0 %all-gather.39.cloned.1.call-start = ((), (), s32[]{:S(2)}) async-start(), calls=%async_computation.3 | async-start | bytes 9437184 | tf_op jit(solution)/shard_map/all_gather | solution.py:64
  15.6 297.8 %all-gather.41.cloned.1.call-start = ((), (), s32[]{:S(2)}) async-start(), calls=%async_computation.4 | async-start | bytes 37748736 | tf_op jit(solution)/shard_map/all_gather | solution.py:64
  21.6 446.8 %all-gather.43.cloned.1.call-start = ((), (), s32[]{:S(2)}) async-start(), calls=%async_computation.5 | async-start | bytes 37748736 | tf_op jit(solution)/shard_map/all_gather | solution.py:64
  27.7 596.0 %all-gather.45.cloned.1.call-start = ((), (), s32[]{:S(2)}) async-start(), calls=%async_computation.6 | async-start | bytes 37748736 | tf_op jit(solution)/shard_map/all_gather | solution.py:64
  33.9 641.1 %all-gather.51.cloned.1.call-start = ((), (), s32[]{:S(2)}) async-start(), calls=%async_computation.9 | async-start | bytes 9437184 | tf_op jit(solution)/shard_map/all_gather | solution.py:64
  34.7 665.1 %all-gather.49.cloned.1.call-start = ((), (), s32[]{:S(2)}) async-start(), calls=%async_computation.8 | async-start | bytes 2359296 | tf_op jit(solution)/shard_map/all_gather | solution.py:64
  35.5 689.0 %all-gather.47.cloned.1.call-start = ((), (), s32[]{:S(2)}) async-start(), calls=%async_computation.7 | async-start | bytes 2359296 | tf_op jit(solution)/shard_map/all_gather | solution.py:64
  36.1 736.3 %all-gather.53.cloned.1.call-start = ((), (), s32[]{:S(2)}) async-start(), calls=%async_computation.10 | async-start | bytes 9437184 | tf_op jit(solution)/shard_map/all_gather | solution.py:64
  36.9 890.0 %all-gather.55.cloned.1.call-start = ((), (), s32[]{:S(2)}) async-start(), calls=%async_computation.11 | async-start | bytes 37748736 | tf_op jit(solution)/shard_map/all_gather | solution.py:64
  37.6 1044.5 %all-gather.57.cloned.1.call-start = ((), (), s32[]{:S(2)}) async-start(), calls=%async_computation.12 | async-start | bytes 37748736 | tf_op jit(solution)/shard_map/all_gather | solution.py:64
  37.6 1.4 copy-start.2
  37.6 20.7 %copy-start.3 = (bf16[2,256]{1,0:T(2,128)(2,1)S(1)}, bf16[2,256]{1,0:T(2,128)(2,1)}, u32[]{:S(2)}) copy-start(bf16[2,256]{1,0:T(2,128)(2,1)} %param.16) | copy-start | bytes 3076
  37.7 85.9 %copy-start = (bf16[1,64,2048]{2,1,0:T(8,128)(2,1)S(1)}, bf16[1,64,2048]{2,1,0:T(8,128)(2,1)}, u32[]{:S(2)}) copy-start(bf16[1,64,2048]{2,1,0:T(8,128)(2,1)} %param.10) | copy-start | bytes 786436
  38.4 1198.8 %all-gather.59.cloned.1.call-start = ((), (), s32[]{:S(2)}) async-start(), calls=%async_computation.13 | async-start | bytes 37748736 | tf_op jit(solution)/shard_map/all_gather | solution.py:64
Sparse Core Ops, SparseCore 0:
  8.9 25.6 all-gather.34
  36.1 23.2 all-gather.32
  61.1 50.0 all-gather.36
  112.6 46.3 all-gather.38
  160.4 152.9 all-gather.40
  314.8 153.5 all-gather.42
  470.0 153.5 all-gather.44
  625.2 49.6 all-gather.50
  676.5 23.2 all-gather.48
  701.2 23.2 all-gather.46
  726.1 46.3 all-gather.52
  773.9 152.9 all-gather.54
  928.5 153.5 all-gather.56
  1083.5 153.5 all-gather.58
where the time goes:
time: 1270 us
  waiting for transfers between devices  1030 us (81%)
  matrix products  111 us (9%)
  blocking collectives  84.5 us (7%)
  local copies, waits for them, and re-layouts  27.6 us (2%)
  between operations  13.6 us (1%)
    all_gather x14, waiting for transfers between devices, local_forward(): lax.all_gather(shard[layer], 'fsdp', axis=0, tiled=True)  1030 us
    all_gather x4, blocking collectives, local_forward(): lax.all_gather(shard[layer], 'fsdp', axis=0, tiled=True)  84.5 us
    dot_general x2, matrix products, decoder_layer(): jnp.einsum('bsf,fd->bsd', gated, w_down, preferred_element_type=jnp.float32)  50.2 us
    dot_general x2, matrix products, decoder_layer(): jnp.einsum('bsd,df->bsf', mlp_in, w_gate, preferred_element_type=jnp.floa...  27.2 us
    slice x9, local copies, waits for them, and re-layouts, local_forward(): shard[layer]  26.4 us
  transfers between devices with their start and end apart: 14, of which 11 were waited for; matrix products, arithmetic and copies ran while one was open for 9% of the time, Pallas kernels for 0%

commit v1 on v0

v1 whole, which is shorter than its diff:
```python
import functools

import jax
import jax.numpy as jnp
import numpy as np
from jax import lax
from jax.experimental import pallas as pl
from jax.experimental.pallas import tpu as pltpu
from jax.sharding import PartitionSpec as P

ROPE_THETA = 500000.0
NORM_EPS = 1e-5
MESH = pl.DeviceIdType.MESH
F32 = jnp.float32
BF16 = jnp.bfloat16

QKV, WO, GATE, UP = range(4)
AX, AO, AM = range(3)
REMOTE = (2, 3, 6, 7, 4, 5)
TAKE = ((256, 128, 128, 128), (128, 128, 128, 128))


def kernel(n, x_hbm, an_ref, mn_ref, tab_hbm, wq, wk, wv, wo, wg, wu, wd, y_ref,
           xf, of, x1f, uf, qkvf, zf, gains, tab, wqkv_v, wo_v, wg_v, wu_v, wd_v, psib, pown, rsib, rrem,
           sw, rw, sf, rf, sa, ra, sg, rg, ss, rs, sr, rr, lsem):
    chips = n // 2
    dp, f = lax.axis_index("dp"), lax.axis_index("fsdp")
    c, k = f // 2, lax.rem(f, 2)
    par = lax.rem(dp, 2)
    partner = dp + 1 - 2 * par
    layers, seq, width = 2, x_hbm.shape[0], x_hbm.shape[1]
    blk = width // n
    tokens = n * seq
    half = tokens // 2
    ffn = wg_v.shape[2]
    heads = 4
    hd = blk // heads

    def chip(d):
        return lax.rem(c + d + chips, chips)

    def to(i):
        return (dp, chip(i // 2) * 2 + lax.rem(k + i % 2, 2))

    def source(i):
        return chip(-(i // 2)) * 2 + lax.rem(k + i % 2, 2)

    def al(v, m):
        return pl.multiple_of(v, m)

    def rc(src, dst, ssem, rsem, dev):
        return pltpu.make_async_remote_copy(src_ref=src, dst_ref=dst, send_sem=ssem, recv_sem=rsem, device_id=dev, device_id_type=MESH)

    def taken(sem, ref):
        pltpu.make_async_copy(ref, ref, sem).wait()

    def block(l, g, src, r0, rows):
        if g == QKV:
            return wqkv_v.at[l, :, pl.ds(al(src * blk + r0, 128), rows)]
        return (None, wo_v, wg_v, wu_v)[g].at[l, pl.ds(al(src * blk + r0, 16), rows), :]

    def pieces(l, g, dst, src, r0, rows):
        if g == QKV:
            cols = pl.ds(al(src * blk + r0, 128), rows)
            mine = pl.ds(al(r0, 128), rows)
            kvd = wk.shape[1] // n
            return [(wq.at[l, pl.ds(al(dst * blk, 16), blk), mine], wqkv_v.at[l, pl.ds(0, blk), cols]),
                    (wk.at[l, pl.ds(al(dst * kvd, 16), kvd), mine], wqkv_v.at[l, pl.ds(blk, kvd), cols]),
                    (wv.at[l, pl.ds(al(dst * kvd, 16), kvd), mine], wqkv_v.at[l, pl.ds(blk + kvd, kvd), cols])]
        w, wide = ((None, None), (wo, blk), (wg, ffn), (wu, ffn))[g]
        return [(w.at[l, pl.ds(al(r0, 16), rows), pl.ds(al(dst * wide, 128), wide)], block(l, g, src, r0, rows))]

    def bytes_of(l, g, rows):
        if g == QKV:
            return wqkv_v.at[l, :, pl.ds(0, rows)]
        return (None, wo_v, wg_v, wu_v)[g].at[l, pl.ds(0, rows), :]

    def issue(l, g, idx):
        for i in idx:
            rows = blk if i == 1 else TAKE[l][g]
            r0 = par * (blk - rows)
            dst = to(i)
            for a, b in pieces(l, g, dst[1], f, r0, rows):
                rc(a, b, sw.at[l, g], rw.at[l, g, i], dst).start()

    def own(l, g):
        for a, b in pieces(l, g, f, f, 0, blk):
            pltpu.make_async_copy(a, b, lsem.at[l, g]).start()

    def arrived(l, g, i):
        rows = blk if i == 1 else TAKE[l][g]
        taken(rw.at[l, g, i], block(l, g, source(i), par * (blk - rows), rows))

    def forward(l, g, idx):
        rows = TAKE[l][g]
        for i in idx:
            arrived(l, g, i)
            if rows < blk:
                there = block(l, g, source(i), par * rows, blk - rows)
                rc(there, there, sf.at[l, g], rf.at[l, g], (partner, f)).start()

    def complete(l, g):
        taken(lsem.at[l, g], bytes_of(l, g, blk))
        arrived(l, g, 1)
        if TAKE[l][g] < blk:
            taken(rf.at[l, g], bytes_of(l, g, len(REMOTE) * (blk - TAKE[l][g])))

    def part(a, src):
        if a == AX:
            return xf.at[pl.ds(al((lax.rem(src, 2) * chips + src // 2) * seq, seq), seq), :]
        return (None, of, x1f)[a].at[:, pl.ds(al(src * blk, 128), blk)]

    def gather_start(l, a, mine=None):
        mine = part(a, f) if mine is None else mine
        for i in (2, 6, 4, 1):
            rc(mine, part(a, f), sa.at[l, a, i], ra.at[l, a, i], to(i)).start()

    def gather_pass(l, a):
        for i in (2, 6, 4):
            got = part(a, source(i))
            taken(ra.at[l, a, i], got)
            rc(got, got, sa.at[l, a, i + 1], ra.at[l, a, i + 1], to(1)).start()

    def gather_end(l, a):
        for i in (1, 3, 7, 5):
            taken(ra.at[l, a, i], part(a, source(i)))
        for i in range(1, n):
            taken(sa.at[l, a, i], part(a, f))

    def norm(src, row):
        step = 32
        gain = gains[pl.ds(row, 1), :]

        @pl.loop(0, tokens // step)
        def _(i):
            at = pl.ds(al(i * step, step), step)
            v = src[at, :].astype(F32)
            inv = lax.rsqrt(jnp.mean(v * v, axis=-1, keepdims=True) + NORM_EPS)
            uf[at, :] = (v * inv * gain).astype(BF16)

    def project(l):
        step = 256

        @pl.loop(0, tokens // step)
        def _(i):
            at = pl.ds(al(i * step, step), step)
            qkvf[at, :] = lax.dot_general(uf[at, :], wqkv_v[l], (((1,), (1,)), ((), ())), preferred_element_type=F32)

    def attend():
        lane = lax.broadcasted_iota(jnp.int32, (seq, 128), 1)
        low = lax.rem(lane, hd) < hd // 2
        first = lane < hd
        head = lax.broadcasted_iota(jnp.int32, (seq, blk), 1) // hd
        qpos = lax.rem(lax.broadcasted_iota(jnp.int32, (heads * seq, seq), 0), seq)
        seen = qpos >= lax.broadcasted_iota(jnp.int32, (heads * seq, seq), 1)

        def rope(v):
            turned = jnp.where(low, pltpu.roll(v, 128 - hd // 2, 1), pltpu.roll(v, hd // 2, 1))
            return v * tab[0] + turned * tab[1]

        @pl.loop(0, n)
        def _(s):
            at = pl.ds(al(s * seq, seq), seq)
            q = jnp.concatenate([rope(qkvf[at, 0:128]), rope(qkvf[at, 128:256])], axis=1)
            kv = qkvf[at, 256:384]
            kr = rope(kv)
            k2 = jnp.where(first, kr, pltpu.roll(kr, hd, 1)).astype(BF16)
            v2 = jnp.where(first, pltpu.roll(kv, hd, 1), kv).astype(BF16)
            k4 = jnp.concatenate([k2, k2], axis=1)
            v4 = jnp.concatenate([v2, v2], axis=1)
            q4 = jnp.concatenate([jnp.where(head == h, q, 0.0) for h in range(heads)], axis=0).astype(BF16)
            score = lax.dot_general(q4, k4, (((1,), (1,)), ((), ())), preferred_element_type=F32) * hd ** -0.5
            score = jnp.where(seen, score, -jnp.inf)
            e = jnp.exp(score - jnp.max(score, axis=-1, keepdims=True))
            prob = (e / jnp.sum(e, axis=-1, keepdims=True)).astype(BF16)
            o4 = jnp.dot(prob, v4, preferred_element_type=F32)
            o = o4[0:seq]
            for h in range(1, heads):
                o = jnp.where(head == h, o4[h * seq:(h + 1) * seq], o)
            of[at, pl.ds(al(f * blk, 128), blk)] = o.astype(BF16)

    def output_projection(l):
        step = 256

        @pl.loop(0, tokens // step)
        def _(i):
            at = pl.ds(al(i * step, step), step)
            cols = pl.ds(al(f * blk, 128), blk)
            acc = jnp.dot(of[at, :], wo_v[l], preferred_element_type=F32)
            x1f[at, cols] = (xf[at, cols].astype(F32) + acc).astype(BF16)

    def gate_up(l):
        step = 256

        @pl.loop(0, ffn // step)
        def _(i):
            at = pl.ds(al(i * step, step), step)
            a = jnp.dot(uf[...], wg_v[l, :, at], preferred_element_type=F32).astype(BF16).astype(F32)
            b = jnp.dot(uf[...], wu_v[l, :, at], preferred_element_type=F32).astype(BF16).astype(F32)
            zf[:, at] = (a * jax.nn.sigmoid(a) * b).astype(BF16)

    dtile = psib.shape[1] // 4

    def down_start(l):
        for t in range(4):
            cols = pl.ds(t * dtile, dtile)
            psib[:, cols] = jnp.dot(zf[pl.ds(al((1 - k) * half, half), half), :], wd_v[l, :, cols], preferred_element_type=F32)
            rc(psib.at[:, cols], rsib.at[:, cols], ss.at[l, t], rs.at[l, t], to(1)).start()
        for t in range(4):
            cols = pl.ds(t * dtile, dtile)
            acc = jnp.dot(zf[pl.ds(al(k * half, half), half), :], wd_v[l, :, cols], preferred_element_type=F32)
            taken(rs.at[l, t], rsib.at[:, cols])
            pown[:, cols] = acc + rsib[:, cols]
            for d in (1, 3, 2):
                rows = pl.ds(al(chip(d) * seq, seq), seq)
                rc(pown.at[rows, cols], rrem.at[d, :, cols], sr.at[l, t, d], rr.at[l, t, d], to(2 * d)).start()

    def down_end(l, out):
        mine = pl.ds(al(c * seq, seq), seq)
        at = pl.ds(al((k * chips + c) * seq, seq), seq)
        for t in range(4):
            cols = pl.ds(t * dtile, dtile)
            for d in (1, 3, 2):
                taken(rr.at[l, t, d], rrem.at[d, :, cols])
            acc = pown[mine, cols] + rrem[1, :, cols] + (rrem[3, :, cols] + rrem[2, :, cols])
            out(cols, (x1f[at, cols].astype(F32) + acc).astype(BF16))

    def down_sent(l):
        for t in range(4):
            cols = pl.ds(t * dtile, dtile)
            taken(ss.at[l, t], psib.at[:, cols])
            for d in (1, 3, 2):
                taken(sr.at[l, t, d], rrem.at[d, :, cols])

    gains[...] = jnp.zeros_like(gains)
    mycols = pl.ds(al(f * blk, 128), blk)
    gains[0:2, mycols] = an_ref[...].astype(F32)
    gains[2:4, mycols] = mn_ref[...].astype(F32)
    gblock = gains.at[:, mycols]
    local_x = pltpu.make_async_copy(x_hbm, part(AX, f), lsem.at[0, 4])
    local_x.start()
    local_tab = pltpu.make_async_copy(tab_hbm, tab, lsem.at[1, 4])
    local_tab.start()
    own(0, QKV)

    barrier = pltpu.get_barrier_semaphore()
    for i in range(1, n):
        pl.semaphore_signal(barrier, inc=1, device_id=to(i), device_id_type=MESH)
    pl.semaphore_signal(barrier, inc=1, device_id=(partner, f), device_id_type=MESH)
    pl.semaphore_wait(barrier, n)

    gather_start(0, AX, x_hbm)
    issue(0, QKV, REMOTE + (1,))
    for i in range(1, n):
        rc(gblock, gblock, sg.at[i], rg.at[i], to(i)).start()
    for g in (WO, GATE, UP):
        own(0, g)
    issue(0, WO, REMOTE + (1,))
    issue(0, GATE, REMOTE[:4] + (1,))
    own_d = [pltpu.make_async_copy(wd.at[l], wd_v.at[l], lsem.at[l, 5]) for l in range(layers)]
    own_d[0].start()

    for l in range(layers):
        if l == 0:
            local_x.wait()
            local_tab.wait()
            for i in range(1, n):
                taken(rg.at[i], gains.at[:, pl.ds(al(source(i) * blk, 128), blk)])
        gather_pass(l, AX)
        gather_end(l, AX)
        norm(xf, l)
        if TAKE[l][QKV] == blk:
            forward(l, QKV, REMOTE)
        complete(l, QKV)
        project(l)
        attend()
        gather_start(l, AO)
        issue(l, GATE, REMOTE[4:])
        issue(l, UP, REMOTE[:4] + (1,))
        forward(l, WO, REMOTE)
        forward(l, GATE, REMOTE[:4])
        gather_pass(l, AO)
        gather_end(l, AO)
        complete(l, WO)
        output_projection(l)
        gather_start(l, AM)
        issue(l, UP, REMOTE[4:])
        forward(l, GATE, REMOTE[4:])
        forward(l, UP, REMOTE[:4])
        gather_pass(l, AM)
        gather_end(l, AM)
        norm(x1f, layers + l)
        forward(l, UP, REMOTE[4:])
        if l + 1 < layers:
            issue(l + 1, QKV, REMOTE + (1,))
            for g in range(4):
                own(l + 1, g)
            own_d[l + 1].start()
        complete(l, GATE)
        complete(l, UP)
        gate_up(l)
        own_d[l].wait()
        down_start(l)
        if l + 1 < layers:
            issue(l + 1, WO, REMOTE + (1,))
            forward(l + 1, QKV, REMOTE)

            def store(cols, v):
                xf[pl.ds(al((k * chips + c) * seq, seq), seq), cols] = v

            down_end(l, store)
            down_sent(l)
            gather_start(l + 1, AX)
            issue(l + 1, GATE, REMOTE[:4] + (1,))
        else:
            def store(cols, v):
                y_ref[:, cols] = v

            down_end(l, store)
            down_sent(l)

    for i in range(1, n):
        taken(sg.at[i], gblock)
    for l in range(layers):
        for g in range(4):
            taken(sw.at[l, g], bytes_of(l, g, len(REMOTE) * TAKE[l][g] + blk))
            if TAKE[l][g] < blk:
                taken(sf.at[l, g], bytes_of(l, g, len(REMOTE) * (blk - TAKE[l][g])))


def rope_tables(seq, hd):
    inv_freq = np.power(np.float32(ROPE_THETA), -(np.arange(hd // 2, dtype=np.float32) * np.float32(2.0) / np.float32(hd)))
    angles = np.arange(seq, dtype=np.float32)[:, None] * inv_freq[None, :].astype(np.float32)
    cos, sin = np.cos(angles), np.sin(angles)
    cos = np.concatenate([cos, cos] * (128 // hd), axis=1)
    sin = np.concatenate([-sin, sin] * (128 // hd), axis=1)
    return np.stack([cos, sin]).astype(np.float32)


def solution(mesh):
    n = mesh.shape["fsdp"]
    batch_spec = P(("dp", "fsdp"), None, None)
    gain_spec = P(None, "fsdp")
    proj_spec = P(None, "fsdp", None, None)
    mat_spec = P(None, "fsdp", None)

    def local_forward(hidden, attn_norm, w_q, w_k, w_v, w_o, mlp_norm, w_gate, w_up, w_down):
        seq, width = hidden.shape[1], hidden.shape[2]
        layers, blk, hd = w_q.shape[0], w_q.shape[1], w_q.shape[3]
        tokens, ffn = n * seq, w_gate.shape[2] // n
        half = tokens // 2
        qkv = (w_q.shape[2] + 2 * w_k.shape[2]) * hd // n

        def turn(w):
            return jnp.transpose(w, (0, 2, 3, 1)).reshape(layers, w.shape[2] * hd, blk)

        tables = jnp.asarray(rope_tables(seq, hd))
        anyspace = pl.BlockSpec(memory_space=pl.ANY)
        vmem = pl.BlockSpec(memory_space=pltpu.VMEM)
        dma = pltpu.SemaphoreType.DMA
        out = pl.pallas_call(
            functools.partial(kernel, n),
            out_shape=jax.ShapeDtypeStruct((seq, width), BF16),
            in_specs=[anyspace, vmem, vmem] + [anyspace] * 8,
            out_specs=vmem,
            scratch_shapes=[
                pltpu.VMEM((tokens, width), BF16),
                pltpu.VMEM((tokens, width), BF16),
                pltpu.VMEM((tokens, width), BF16),
                pltpu.VMEM((tokens, width), BF16),
                pltpu.VMEM((tokens, qkv), F32),
                pltpu.VMEM((tokens, ffn), BF16),
                pltpu.VMEM((8, width), F32),
                pltpu.VMEM((2, seq, 128), F32),
                pltpu.VMEM((layers, qkv, width), BF16),
                pltpu.VMEM((layers, width, blk), BF16),
                pltpu.VMEM((layers, width, ffn), BF16),
                pltpu.VMEM((layers, width, ffn), BF16),
                pltpu.VMEM((layers, ffn, width), BF16),
                pltpu.VMEM((half, width), F32),
                pltpu.VMEM((half, width), F32),
                pltpu.VMEM((half, width), F32),
                pltpu.VMEM((4, seq, width), F32),
                dma((layers, 4)), dma((layers, 4, n)),
                dma((layers, 4)), dma((layers, 4)),
                dma((layers, 3, n)), dma((layers, 3, n)),
                dma((n,)), dma((n,)),
                dma((layers, 4)), dma((layers, 4)),
                dma((layers, 4, 4)), dma((layers, 4, 4)),
                dma((layers, 6)),
            ],
            compiler_params=pltpu.CompilerParams(collective_id=0, has_side_effects=True, vmem_limit_bytes=63 * 2**20),
        )(hidden[0], attn_norm, mlp_norm, tables, turn(w_q), turn(w_k), turn(w_v), w_o, w_gate, w_up, w_down)
        return out[None]

    return jax.shard_map(local_forward, mesh=mesh, in_specs=(batch_spec, gain_spec, proj_spec, proj_spec, proj_spec, mat_spec, gain_spec, mat_spec, mat_spec, mat_spec), out_specs=batch_spec, check_vma=False)
```

time: 1270 us -> 304 us (0.24)
  waiting for transfers between devices: 1030 us -> 0 us
  Pallas kernels: 0 us -> 302 us
  matrix products: 111 us -> 0 us
  blocking collectives: 84.5 us -> 0 us
  local copies, waits for them, and re-layouts: 27.6 us -> 1.67 us
  between operations: 13.6 us -> 0.01 us
    all_gather x14 -> x0, waiting for transfers between devices: 1030 us -> none  [local_forward(): lax.all_gather(shard[layer], 'fsdp', axis=0, tiled=True)]
    pallas_call x0 -> x1, Pallas kernels: none -> 302 us  [local_forward(): pl.pallas_call(functools.partial(kernel, n), out_shape=jax.ShapeDtypeStru...]
    dot_general x10 -> x0, matrix products: 89.7 us -> none  [the longest x2 50.2 us: decoder_layer(): jnp.einsum('bsf,fd->bsd', gated, w_down, preferred_element_type=jnp.float32)]
    all_gather x4 -> x0, blocking collectives: 84.5 us -> none  [local_forward(): lax.all_gather(shard[layer], 'fsdp', axis=0, tiled=True)]
    slice x9 -> x0, local copies, waits for them, and re-layouts: 26.4 us -> none  [local_forward(): shard[layer]]
    unnamed x6 -> x0, matrix products: 20.8 us -> none
  transfers between devices with their start and end apart: 14 -> 0, of which waited for: 11 -> 0; matrix products, arithmetic and copies ran while one was open for 9% -> 0% of each run, Pallas kernels for 0% -> 0%
where the time goes in v1:
time: 304 us
  Pallas kernels  302 us (99%)
    pallas_call x1, Pallas kernels, local_forward(): pl.pallas_call(functools.partial(kernel, n), out_shape=jax.ShapeDtypeStru...  302 us

profile of v1, /device:TPU:113, one launch (start us, length us, event | category | flops | bytes accessed | tf_op | source)
XLA Modules:
  0.0 303.5 jit_solution(7515285874359300502)
XLA Ops:
  0.0 301.8 %shard_map.109 = bf16[64,2048]{1,0:T(8,128)(2,1)} custom-call(bf16[64,2048]{1,0:T(8,128)(2,1)} %bitcast.15, bf16[2,256]{1,0:T(2,128)(2,1)} %an_ref.1, bf16[2,256]{1,0:T(2,128)(2,1)} %mn_ref.1, f32[2,64,128]{2,1,0:T(8,128)} %constant.2.clone.tab_hbm, bf16[2,2048,256]{2,1,0:T(8,128)(2,1)} %bitcast.11, bf16[2,512,256]{2,1,0:T(8,128)(2,1)} %bitcast.13, ...), custom_call_target="tpu_custom_call" | custom-call | tf_op jit(solution)/shard_map/pallas_call | solution.py:361
  301.8 1.7 copy.13

commit v2 on v1

--- a/solution.py
+++ b/solution.py
@@ -14,10 +14,15 @@
 F32 = jnp.float32
 BF16 = jnp.bfloat16
 
-QKV, WO, GATE, UP = range(4)
+QKV, WO, G0, G1, U0, U1 = range(6)
 AX, AO, AM = range(3)
 REMOTE = (2, 3, 6, 7, 4, 5)
-TAKE = ((256, 128, 128, 128), (128, 128, 128, 128))
+SAME, CROSS, NEAR, FAR = (2, 6), (3, 7), REMOTE[:4], REMOTE[4:] + (1,)
+ALL = REMOTE + (1,)
+GROUPS = 6
+SPLIT = 4
+TILES = 8
+TAKE = ((128, 128, 128, 128, 128, 128), (128, 128, 128, 128, 128, 128))
 
 
 def kernel(n, x_hbm, an_ref, mn_ref, tab_hbm, wq, wk, wv, wo, wg, wu, wd, y_ref,
@@ -33,6 +38,7 @@
     tokens = n * seq
     half = tokens // 2
     ffn = wg_v.shape[2]
+    part_w = ffn // 2
     heads = 4
     hd = blk // heads
 
@@ -57,7 +63,9 @@
     def block(l, g, src, r0, rows):
         if g == QKV:
             return wqkv_v.at[l, :, pl.ds(al(src * blk + r0, 128), rows)]
-        return (None, wo_v, wg_v, wu_v)[g].at[l, pl.ds(al(src * blk + r0, 16), rows), :]
+        if g == WO:
+            return wo_v.at[l, pl.ds(al(src * blk + r0, 16), rows), :]
+        return (wg_v, wu_v)[(g - G0) // 2].at[l, pl.ds(al(src * blk + r0, 16), rows), pl.ds((g - G0) % 2 * part_w, part_w)]
 
     def pieces(l, g, dst, src, r0, rows):
         if g == QKV:
@@ -67,13 +75,15 @@
             return [(wq.at[l, pl.ds(al(dst * blk, 16), blk), mine], wqkv_v.at[l, pl.ds(0, blk), cols]),
                     (wk.at[l, pl.ds(al(dst * kvd, 16), kvd), mine], wqkv_v.at[l, pl.ds(blk, kvd), cols]),
                     (wv.at[l, pl.ds(al(dst * kvd, 16), kvd), mine], wqkv_v.at[l, pl.ds(blk + kvd, kvd), cols])]
-        w, wide = ((None, None), (wo, blk), (wg, ffn), (wu, ffn))[g]
-        return [(w.at[l, pl.ds(al(r0, 16), rows), pl.ds(al(dst * wide, 128), wide)], block(l, g, src, r0, rows))]
+        w, at, wide = (wo, dst * blk, blk) if g == WO else ((wg, wu)[(g - G0) // 2], dst * ffn + (g - G0) % 2 * part_w, part_w)
+        return [(w.at[l, pl.ds(al(r0, 16), rows), pl.ds(al(at, 128), wide)], block(l, g, src, r0, rows))]
 
     def bytes_of(l, g, rows):
         if g == QKV:
             return wqkv_v.at[l, :, pl.ds(0, rows)]
-        return (None, wo_v, wg_v, wu_v)[g].at[l, pl.ds(0, rows), :]
+        if g == WO:
+            return wo_v.at[l, pl.ds(0, rows), :]
+        return (wg_v, wu_v)[(g - G0) // 2].at[l, pl.ds(0, rows), pl.ds((g - G0) % 2 * part_w, part_w)]
 
     def issue(l, g, idx):
         for i in idx:
@@ -91,9 +101,11 @@
         rows = blk if i == 1 else TAKE[l][g]
         taken(rw.at[l, g, i], block(l, g, source(i), par * (blk - rows), rows))
 
-    def forward(l, g, idx):
+    def forward(l, g, idx=REMOTE):
         rows = TAKE[l][g]
         for i in idx:
+            if i == 1:
+                continue
             arrived(l, g, i)
             if rows < blk:
                 there = block(l, g, source(i), par * rows, blk - rows)
@@ -110,22 +122,41 @@
             return xf.at[pl.ds(al((lax.rem(src, 2) * chips + src // 2) * seq, seq), seq), :]
         return (None, of, x1f)[a].at[:, pl.ds(al(src * blk, 128), blk)]
 
+    def piece(a, src, i, m):
+        if a == AX:
+            return xf.at[pl.ds(al((lax.rem(src, 2) * chips + src // 2) * seq + i * (seq // m), seq // m), seq // m), :]
+        return (None, of, x1f)[a].at[pl.ds(i * (tokens // m), tokens // m), pl.ds(al(src * blk, 128), blk)]
+
     def gather_start(l, a, mine=None):
-        mine = part(a, f) if mine is None else mine
-        for i in (2, 6, 4, 1):
-            rc(mine, part(a, f), sa.at[l, a, i], ra.at[l, a, i], to(i)).start()
-
-    def gather_pass(l, a):
-        for i in (2, 6, 4):
+        for q in range(SPLIT):
+            for i in (2, 6):
+                to_here = piece(a, f, q, SPLIT)
+                from_here = to_here if mine is None else mine.at[pl.ds(q * (seq // SPLIT), seq // SPLIT), :]
+                rc(from_here, to_here, sa.at[l, a, i], ra.at[l, a, i], to(i)).start()
+        rc(part(a, f) if mine is None else mine, part(a, f), sa.at[l, a, 1], ra.at[l, a, 1], to(1)).start()
+
+    def gather_near(l, a):
+        for i, h, j in ((2, 0, 4), (6, 1, 0)):
             got = part(a, source(i))
             taken(ra.at[l, a, i], got)
+            for q in range(SPLIT // 2):
+                on = piece(a, source(i), h * (SPLIT // 2) + q, SPLIT)
+                rc(on, on, sa.at[l, a, j], ra.at[l, a, j], to(i)).start()
             rc(got, got, sa.at[l, a, i + 1], ra.at[l, a, i + 1], to(1)).start()
+
+    def gather_far(l, a):
+        for j, h in ((4, 0), (0, 1)):
+            taken(ra.at[l, a, j], piece(a, source(4), h, 2))
+        got = part(a, source(4))
+        rc(got, got, sa.at[l, a, 5], ra.at[l, a, 5], to(1)).start()
 
     def gather_end(l, a):
         for i in (1, 3, 7, 5):
             taken(ra.at[l, a, i], part(a, source(i)))
-        for i in range(1, n):
+        for i in (1, 2, 3, 5, 6, 7):
             taken(sa.at[l, a, i], part(a, f))
+        for j in (0, 4):
+            taken(sa.at[l, a, j], piece(a, f, 0, 2))
 
     def norm(src, row):
         step = 32
@@ -146,7 +177,7 @@
             at = pl.ds(al(i * step, step), step)
             qkvf[at, :] = lax.dot_general(uf[at, :], wqkv_v[l], (((1,), (1,)), ((), ())), preferred_element_type=F32)
 
-    def attend():
+    def attend(lo, hi):
         lane = lax.broadcasted_iota(jnp.int32, (seq, 128), 1)
         low = lax.rem(lane, hd) < hd // 2
         first = lane < hd
@@ -158,7 +189,7 @@
             turned = jnp.where(low, pltpu.roll(v, 128 - hd // 2, 1), pltpu.roll(v, hd // 2, 1))
             return v * tab[0] + turned * tab[1]
 
-        @pl.loop(0, n)
+        @pl.loop(lo, hi)
         def _(s):
             at = pl.ds(al(s * seq, seq), seq)
             q = jnp.concatenate([rope(qkvf[at, 0:128]), rope(qkvf[at, 128:256])], axis=1)
@@ -189,17 +220,31 @@
             acc = jnp.dot(of[at, :], wo_v[l], preferred_element_type=F32)
             x1f[at, cols] = (xf[at, cols].astype(F32) + acc).astype(BF16)
 
-    def gate_up(l):
+    def gate_up(l, h):
         step = 256
 
-        @pl.loop(0, ffn // step)
+        @pl.loop(h * part_w // step, (h + 1) * part_w // step)
         def _(i):
             at = pl.ds(al(i * step, step), step)
             a = jnp.dot(uf[...], wg_v[l, :, at], preferred_element_type=F32).astype(BF16).astype(F32)
             b = jnp.dot(uf[...], wu_v[l, :, at], preferred_element_type=F32).astype(BF16).astype(F32)
             zf[:, at] = (a * jax.nn.sigmoid(a) * b).astype(BF16)
 
-    dtile = psib.shape[1] // 4
+    dtile = width // 4
+    ptile = width // TILES
+    per = TILES // 4
+
+    def pcols(p):
+        return pl.ds(p * ptile, ptile)
+
+    def side(p):
+        return 2 * p % 4 - 1
+
+    def hop(s):
+        return 2 if s == 1 else 6
+
+    def rows_of(d):
+        return pl.ds(al(chip(d) * seq, seq), seq)
 
     def down_start(l):
         for t in range(4):
@@ -211,35 +256,41 @@
             acc = jnp.dot(zf[pl.ds(al(k * half, half), half), :], wd_v[l, :, cols], preferred_element_type=F32)
             taken(rs.at[l, t], rsib.at[:, cols])
             pown[:, cols] = acc + rsib[:, cols]
-            for d in (1, 3, 2):
-                rows = pl.ds(al(chip(d) * seq, seq), seq)
-                rc(pown.at[rows, cols], rrem.at[d, :, cols], sr.at[l, t, d], rr.at[l, t, d], to(2 * d)).start()
+            for p in range(t * per, (t + 1) * per):
+                s = side(p)
+                rc(pown.at[rows_of(2), pcols(p)], rrem.at[0, :, pcols(p)], sr.at[l, p, 0], rr.at[l, p, 0], to(hop(s))).start()
+                rc(pown.at[rows_of(-s), pcols(p)], rrem.at[1, :, pcols(p)], sr.at[l, p, 1], rr.at[l, p, 1], to(hop(-s))).start()
+
+    def down_pass(l):
+        for p in range(TILES):
+            s = side(p)
+            taken(rr.at[l, p, 0], rrem.at[0, :, pcols(p)])
+            pown[rows_of(s), pcols(p)] += rrem[0, :, pcols(p)]
+            rc(pown.at[rows_of(s), pcols(p)], rrem.at[2, :, pcols(p)], sr.at[l, p, 2], rr.at[l, p, 2], to(hop(s))).start()
 
     def down_end(l, out):
-        mine = pl.ds(al(c * seq, seq), seq)
         at = pl.ds(al((k * chips + c) * seq, seq), seq)
-        for t in range(4):
-            cols = pl.ds(t * dtile, dtile)
-            for d in (1, 3, 2):
-                taken(rr.at[l, t, d], rrem.at[d, :, cols])
-            acc = pown[mine, cols] + rrem[1, :, cols] + (rrem[3, :, cols] + rrem[2, :, cols])
-            out(cols, (x1f[at, cols].astype(F32) + acc).astype(BF16))
+        for p in range(TILES):
+            for j in (1, 2):
+                taken(rr.at[l, p, j], rrem.at[j, :, pcols(p)])
+            acc = pown[rows_of(0), pcols(p)] + rrem[1, :, pcols(p)] + rrem[2, :, pcols(p)]
+            out(pcols(p), (x1f[at, pcols(p)].astype(F32) + acc).astype(BF16))
 
     def down_sent(l):
         for t in range(4):
-            cols = pl.ds(t * dtile, dtile)
-            taken(ss.at[l, t], psib.at[:, cols])
-            for d in (1, 3, 2):
-                taken(sr.at[l, t, d], rrem.at[d, :, cols])
+            taken(ss.at[l, t], psib.at[:, pl.ds(t * dtile, dtile)])
+        for p in range(TILES):
+            for j in range(3):
+                taken(sr.at[l, p, j], rrem.at[j, :, pcols(p)])
 
     gains[...] = jnp.zeros_like(gains)
     mycols = pl.ds(al(f * blk, 128), blk)
     gains[0:2, mycols] = an_ref[...].astype(F32)
     gains[2:4, mycols] = mn_ref[...].astype(F32)
     gblock = gains.at[:, mycols]
-    local_x = pltpu.make_async_copy(x_hbm, part(AX, f), lsem.at[0, 4])
+    local_x = pltpu.make_async_copy(x_hbm, part(AX, f), lsem.at[0, 6])
     local_x.start()
-    local_tab = pltpu.make_async_copy(tab_hbm, tab, lsem.at[1, 4])
+    local_tab = pltpu.make_async_copy(tab_hbm, tab, lsem.at[1, 6])
     local_tab.start()
     own(0, QKV)
 
@@ -249,80 +300,125 @@
     pl.semaphore_signal(barrier, inc=1, device_id=(partner, f), device_id_type=MESH)
     pl.semaphore_wait(barrier, n)
 
+    issue(0, WO, ALL)
+    issue(0, G0, ALL)
     gather_start(0, AX, x_hbm)
-    issue(0, QKV, REMOTE + (1,))
     for i in range(1, n):
         rc(gblock, gblock, sg.at[i], rg.at[i], to(i)).start()
-    for g in (WO, GATE, UP):
+    issue(0, QKV, ALL)
+    for g in (WO, G0, G1, U0, U1):
         own(0, g)
-    issue(0, WO, REMOTE + (1,))
-    issue(0, GATE, REMOTE[:4] + (1,))
-    own_d = [pltpu.make_async_copy(wd.at[l], wd_v.at[l], lsem.at[l, 5]) for l in range(layers)]
+    own_d = [pltpu.make_async_copy(wd.at[l], wd_v.at[l], lsem.at[l, 7]) for l in range(layers)]
     own_d[0].start()
+    forward(0, WO)
+    forward(0, G0)
 
     for l in range(layers):
+        last = l + 1 == layers
+        gather_near(l, AX)
         if l == 0:
+            issue(l, G1, ALL)
+            forward(l, QKV)
+            gather_far(l, AX)
             local_x.wait()
             local_tab.wait()
             for i in range(1, n):
                 taken(rg.at[i], gains.at[:, pl.ds(al(source(i) * blk, 128), blk)])
-        gather_pass(l, AX)
+        else:
+            issue(l, G0, CROSS)
+            issue(l, G1, FAR)
+            issue(l, G1, NEAR)
+            gather_far(l, AX)
+            forward(l, G0, NEAR)
         gather_end(l, AX)
         norm(xf, l)
-        if TAKE[l][QKV] == blk:
-            forward(l, QKV, REMOTE)
+        if l == 0:
+            issue(l, U0, ALL)
+            forward(l, G1)
         complete(l, QKV)
         project(l)
-        attend()
+        attend(0, n // 2)
+        if l > 0:
+            forward(l, G1, FAR)
+        attend(n // 2, n)
         gather_start(l, AO)
-        issue(l, GATE, REMOTE[4:])
-        issue(l, UP, REMOTE[:4] + (1,))
-        forward(l, WO, REMOTE)
-        forward(l, GATE, REMOTE[:4])
-        gather_pass(l, AO)
+        if l == 0:
+            issue(l, U1, SAME)
+            forward(l, U0)
+            gather_near(l, AO)
+            issue(l, U1, CROSS)
+            issue(l, U1, FAR)
+            forward(l, U1, SAME)
+            gather_far(l, AO)
+            forward(l, U1, CROSS)
+        else:
+            issue(l, U0, SAME)
+            forward(l, G1, NEAR)
+            gather_near(l, AO)
+            issue(l, U0, CROSS)
+            issue(l, U0, FAR)
+            issue(l, U1, FAR)
+            forward(l, U0, SAME)
+            gather_far(l, AO)
+            forward(l, U0, CROSS)
         gather_end(l, AO)
         complete(l, WO)
         output_projection(l)
         gather_start(l, AM)
-        issue(l, UP, REMOTE[4:])
-        forward(l, GATE, REMOTE[4:])
-        forward(l, UP, REMOTE[:4])
-        gather_pass(l, AM)
+        if l == 0:
+            forward(l, U1, FAR)
+            gather_near(l, AM)
+            for part_of in (NEAR, FAR):
+                issue(l + 1, QKV, part_of)
+                issue(l + 1, WO, part_of)
+            for g in range(GROUPS):
+                own(l + 1, g)
+            own_d[l + 1].start()
+            gather_far(l, AM)
+        else:
+            issue(l, U1, SAME)
+            forward(l, U0, FAR)
+            forward(l, U1, FAR)
+            gather_near(l, AM)
+            issue(l, U1, CROSS)
+            forward(l, U1, SAME)
+            gather_far(l, AM)
+            forward(l, U1, CROSS)
         gather_end(l, AM)
         norm(x1f, layers + l)
-        forward(l, UP, REMOTE[4:])
-        if l + 1 < layers:
-            issue(l + 1, QKV, REMOTE + (1,))
-            for g in range(4):
-                own(l + 1, g)
-            own_d[l + 1].start()
-        complete(l, GATE)
-        complete(l, UP)
-        gate_up(l)
+        complete(l, G0)
+        complete(l, U0)
+        gate_up(l, 0)
+        complete(l, G1)
+        complete(l, U1)
+        gate_up(l, 1)
         own_d[l].wait()
         down_start(l)
-        if l + 1 < layers:
-            issue(l + 1, WO, REMOTE + (1,))
-            forward(l + 1, QKV, REMOTE)
-
+        if not last:
             def store(cols, v):
                 xf[pl.ds(al((k * chips + c) * seq, seq), seq), cols] = v
 
+            forward(l + 1, QKV)
+            forward(l + 1, WO)
+            down_pass(l)
+            issue(l + 1, G0, FAR)
             down_end(l, store)
             down_sent(l)
             gather_start(l + 1, AX)
-            issue(l + 1, GATE, REMOTE[:4] + (1,))
+            issue(l + 1, G0, SAME)
+            forward(l + 1, G0, FAR)
         else:
             def store(cols, v):
                 y_ref[:, cols] = v
 
+            down_pass(l)
             down_end(l, store)
             down_sent(l)
 
     for i in range(1, n):
         taken(sg.at[i], gblock)
     for l in range(layers):
-        for g in range(4):
+        for g in range(GROUPS):
             taken(sw.at[l, g], bytes_of(l, g, len(REMOTE) * TAKE[l][g] + blk))
             if TAKE[l][g] < blk:
                 taken(sf.at[l, g], bytes_of(l, g, len(REMOTE) * (blk - TAKE[l][g])))
@@ -380,14 +476,14 @@
                 pltpu.VMEM((half, width), F32),
                 pltpu.VMEM((half, width), F32),
                 pltpu.VMEM((half, width), F32),
-                pltpu.VMEM((4, seq, width), F32),
-                dma((layers, 4)), dma((layers, 4, n)),
-                dma((layers, 4)), dma((layers, 4)),
+                pltpu.VMEM((3, seq, width), F32),
+                dma((layers, GROUPS)), dma((layers, GROUPS, n)),
+                dma((layers, GROUPS)), dma((layers, GROUPS)),
                 dma((layers, 3, n)), dma((layers, 3, n)),
                 dma((n,)), dma((n,)),
                 dma((layers, 4)), dma((layers, 4)),
-                dma((layers, 4, 4)), dma((layers, 4, 4)),
-                dma((layers, 6)),
+                dma((layers, TILES, 3)), dma((layers, TILES, 3)),
+                dma((layers, 8)),
             ],
             compiler_params=pltpu.CompilerParams(collective_id=0, has_side_effects=True, vmem_limit_bytes=63 * 2**20),
         )(hidden[0], attn_norm, mlp_norm, tables, turn(w_q), turn(w_k), turn(w_v), w_o, w_gate, w_up, w_down)

time: 304 us -> 238 us (0.78)
  Pallas kernels: 302 us -> 237 us
    pallas_call x1, Pallas kernels: 302 us -> 237 us  [local_forward(): pl.pallas_call(functools.partial(kernel, n), out_shape=jax.ShapeDtypeStru...]
where the time goes in v2:
time: 238 us
  Pallas kernels  237 us (100%)
    pallas_call x1, Pallas kernels, local_forward(): pl.pallas_call(functools.partial(kernel, n), out_shape=jax.ShapeDtypeStru...  237 us

profile of v2, /device:TPU:113, one launch (start us, length us, event | category | flops | bytes accessed | tf_op | source)
XLA Modules:
  0.0 238.2 jit_solution(10930093357126353047)
XLA Ops:
  0.0 236.5 %shard_map.109 = bf16[64,2048]{1,0:T(8,128)(2,1)} custom-call(bf16[64,2048]{1,0:T(8,128)(2,1)} %bitcast.15, bf16[2,256]{1,0:T(2,128)(2,1)} %an_ref.1, bf16[2,256]{1,0:T(2,128)(2,1)} %mn_ref.1, f32[2,64,128]{2,1,0:T(8,128)} %constant.2.clone.tab_hbm, bf16[2,2048,256]{2,1,0:T(8,128)(2,1)} %bitcast.11, bf16[2,512,256]{2,1,0:T(8,128)(2,1)} %bitcast.13, ...), custom_call_target="tpu_custom_call" | custom-call | tf_op jit(solution)/shard_map/pallas_call | solution.py:457
  236.5 1.7 copy.13

commit v3 on v2

--- a/solution.py
+++ b/solution.py
@@ -17,16 +17,19 @@
 QKV, WO, G0, G1, U0, U1 = range(6)
 AX, AO, AM = range(3)
 REMOTE = (2, 3, 6, 7, 4, 5)
-SAME, CROSS, NEAR, FAR = (2, 6), (3, 7), REMOTE[:4], REMOTE[4:] + (1,)
-ALL = REMOTE + (1,)
+SAME, CROSS, FAR, OTHER = (2, 6), (3, 7), (4, 5), (1,)
 GROUPS = 6
 SPLIT = 4
 TILES = 8
-TAKE = ((128, 128, 128, 128, 128, 128), (128, 128, 128, 128, 128, 128))
-
-
-def kernel(n, x_hbm, an_ref, mn_ref, tab_hbm, wq, wk, wv, wo, wg, wu, wd, y_ref,
-           xf, of, x1f, uf, qkvf, zf, gains, tab, wqkv_v, wo_v, wg_v, wu_v, wd_v, psib, pown, rsib, rrem,
+SEQS = 2
+NROWS = 32
+STEPS = 4
+AHEAD = 2
+WHOLE = ()
+
+
+def kernel(n, x_hbm, an_ref, mn_ref, tab_hbm, wq, wk, wv, wo, wg, wu, wd, y_hbm,
+           xf, of, x1f, uf, qkvf, zf, gains, tab, wqkv_v, wo_v, wg_v, wu_v, wd_v, yv, psib, pown, rsib, rrem,
            sw, rw, sf, rf, sa, ra, sg, rg, ss, rs, sr, rr, lsem):
     chips = n // 2
     dp, f = lax.axis_index("dp"), lax.axis_index("fsdp")
@@ -85,37 +88,42 @@
             return wo_v.at[l, pl.ds(0, rows), :]
         return (wg_v, wu_v)[(g - G0) // 2].at[l, pl.ds(0, rows), pl.ds((g - G0) % 2 * part_w, part_w)]
 
+    def take(l, g, i):
+        return blk if i == 1 or (l, g, i) in WHOLE else blk // 2
+
+    def brought(l, g):
+        return sum(blk - take(l, g, i) for i in REMOTE)
+
     def issue(l, g, idx):
         for i in idx:
-            rows = blk if i == 1 else TAKE[l][g]
+            rows = take(l, g, i)
             r0 = par * (blk - rows)
             dst = to(i)
             for a, b in pieces(l, g, dst[1], f, r0, rows):
-                rc(a, b, sw.at[l, g], rw.at[l, g, i], dst).start()
+                rc(a, b, sw.at[l, g], rw.at[l, g, slot(i)], dst).start()
 
     def own(l, g):
         for a, b in pieces(l, g, f, f, 0, blk):
             pltpu.make_async_copy(a, b, lsem.at[l, g]).start()
 
-    def arrived(l, g, i):
-        rows = blk if i == 1 else TAKE[l][g]
-        taken(rw.at[l, g, i], block(l, g, source(i), par * (blk - rows), rows))
+    def slot(i):
+        return (0, 0, 0, 1, 2, 2, 0, 1)[i] if i > 1 else 3
+
+    def arrived(l, g, idx):
+        taken(rw.at[l, g, slot(idx[0])], bytes_of(l, g, sum(take(l, g, i) for i in idx)))
 
     def forward(l, g, idx=REMOTE):
-        rows = TAKE[l][g]
+        arrived(l, g, idx)
         for i in idx:
-            if i == 1:
-                continue
-            arrived(l, g, i)
+            rows = take(l, g, i)
             if rows < blk:
                 there = block(l, g, source(i), par * rows, blk - rows)
                 rc(there, there, sf.at[l, g], rf.at[l, g], (partner, f)).start()
 
     def complete(l, g):
         taken(lsem.at[l, g], bytes_of(l, g, blk))
-        arrived(l, g, 1)
-        if TAKE[l][g] < blk:
-            taken(rf.at[l, g], bytes_of(l, g, len(REMOTE) * (blk - TAKE[l][g])))
+        arrived(l, g, OTHER)
+        taken(rf.at[l, g], bytes_of(l, g, brought(l, g)))
 
     def part(a, src):
         if a == AX:
@@ -132,34 +140,31 @@
             for i in (2, 6):
                 to_here = piece(a, f, q, SPLIT)
                 from_here = to_here if mine is None else mine.at[pl.ds(q * (seq // SPLIT), seq // SPLIT), :]
-                rc(from_here, to_here, sa.at[l, a, i], ra.at[l, a, i], to(i)).start()
-        rc(part(a, f) if mine is None else mine, part(a, f), sa.at[l, a, 1], ra.at[l, a, 1], to(1)).start()
+                rc(from_here, to_here, sa.at[a], ra.at[a, i], to(i)).start()
+        rc(part(a, f) if mine is None else mine, part(a, f), sa.at[a], ra.at[a, 1], to(1)).start()
 
     def gather_near(l, a):
         for i, h, j in ((2, 0, 4), (6, 1, 0)):
             got = part(a, source(i))
-            taken(ra.at[l, a, i], got)
+            taken(ra.at[a, i], got)
             for q in range(SPLIT // 2):
                 on = piece(a, source(i), h * (SPLIT // 2) + q, SPLIT)
-                rc(on, on, sa.at[l, a, j], ra.at[l, a, j], to(i)).start()
-            rc(got, got, sa.at[l, a, i + 1], ra.at[l, a, i + 1], to(1)).start()
+                rc(on, on, sa.at[a], ra.at[a, j], to(i)).start()
+            rc(got, got, sa.at[a], ra.at[a, i + 1], to(1)).start()
 
     def gather_far(l, a):
         for j, h in ((4, 0), (0, 1)):
-            taken(ra.at[l, a, j], piece(a, source(4), h, 2))
+            taken(ra.at[a, j], piece(a, source(4), h, 2))
         got = part(a, source(4))
-        rc(got, got, sa.at[l, a, 5], ra.at[l, a, 5], to(1)).start()
+        rc(got, got, sa.at[a], ra.at[a, 5], to(1)).start()
 
     def gather_end(l, a):
         for i in (1, 3, 7, 5):
-            taken(ra.at[l, a, i], part(a, source(i)))
-        for i in (1, 2, 3, 5, 6, 7):
-            taken(sa.at[l, a, i], part(a, f))
-        for j in (0, 4):
-            taken(sa.at[l, a, j], piece(a, f, 0, 2))
+            taken(ra.at[a, i], part(a, source(i)))
+        taken(sa.at[a], xf.at[pl.ds(0, (n - 1) * seq), :] if a == AX else of.at[:, pl.ds(0, (n - 1) * blk)])
 
     def norm(src, row):
-        step = 32
+        step = NROWS
         gain = gains[pl.ds(row, 1), :]
 
         @pl.loop(0, tokens // step)
@@ -189,8 +194,7 @@
             turned = jnp.where(low, pltpu.roll(v, 128 - hd // 2, 1), pltpu.roll(v, hd // 2, 1))
             return v * tab[0] + turned * tab[1]
 
-        @pl.loop(lo, hi)
-        def _(s):
+        def one(s):
             at = pl.ds(al(s * seq, seq), seq)
             q = jnp.concatenate([rope(qkvf[at, 0:128]), rope(qkvf[at, 128:256])], axis=1)
             kv = qkvf[at, 256:384]
@@ -208,7 +212,13 @@
             o = o4[0:seq]
             for h in range(1, heads):
                 o = jnp.where(head == h, o4[h * seq:(h + 1) * seq], o)
-            of[at, pl.ds(al(f * blk, 128), blk)] = o.astype(BF16)
+            return at, o.astype(BF16)
+
+        @pl.loop(lo // SEQS, hi // SEQS)
+        def _(i):
+            done = [one(i * SEQS + j) for j in range(SEQS)]
+            for at, o in done:
+                of[at, pl.ds(al(f * blk, 128), blk)] = o
 
     def output_projection(l):
         step = 256
@@ -230,9 +240,9 @@
             b = jnp.dot(uf[...], wu_v[l, :, at], preferred_element_type=F32).astype(BF16).astype(F32)
             zf[:, at] = (a * jax.nn.sigmoid(a) * b).astype(BF16)
 
-    dtile = width // 4
     ptile = width // TILES
-    per = TILES // 4
+    dtile = width // STEPS
+    per = TILES // STEPS
 
     def pcols(p):
         return pl.ds(p * ptile, ptile)
@@ -247,41 +257,43 @@
         return pl.ds(al(chip(d) * seq, seq), seq)
 
     def down_start(l):
-        for t in range(4):
+        def theirs(t):
             cols = pl.ds(t * dtile, dtile)
             psib[:, cols] = jnp.dot(zf[pl.ds(al((1 - k) * half, half), half), :], wd_v[l, :, cols], preferred_element_type=F32)
-            rc(psib.at[:, cols], rsib.at[:, cols], ss.at[l, t], rs.at[l, t], to(1)).start()
-        for t in range(4):
+            rc(psib.at[:, cols], rsib.at[:, cols], ss, rs.at[t], to(1)).start()
+
+        for t in range(AHEAD):
+            theirs(t)
+        for t in range(STEPS):
             cols = pl.ds(t * dtile, dtile)
             acc = jnp.dot(zf[pl.ds(al(k * half, half), half), :], wd_v[l, :, cols], preferred_element_type=F32)
-            taken(rs.at[l, t], rsib.at[:, cols])
+            taken(rs.at[t], rsib.at[:, cols])
             pown[:, cols] = acc + rsib[:, cols]
             for p in range(t * per, (t + 1) * per):
                 s = side(p)
-                rc(pown.at[rows_of(2), pcols(p)], rrem.at[0, :, pcols(p)], sr.at[l, p, 0], rr.at[l, p, 0], to(hop(s))).start()
-                rc(pown.at[rows_of(-s), pcols(p)], rrem.at[1, :, pcols(p)], sr.at[l, p, 1], rr.at[l, p, 1], to(hop(-s))).start()
+                rc(pown.at[rows_of(2), pcols(p)], rrem.at[0, :, pcols(p)], sr, rr.at[p, 0], to(hop(s))).start()
+                rc(pown.at[rows_of(-s), pcols(p)], rrem.at[1, :, pcols(p)], sr, rr.at[p, 1], to(hop(-s))).start()
+            if t + AHEAD < STEPS:
+                theirs(t + AHEAD)
 
     def down_pass(l):
         for p in range(TILES):
             s = side(p)
-            taken(rr.at[l, p, 0], rrem.at[0, :, pcols(p)])
+            taken(rr.at[p, 0], rrem.at[0, :, pcols(p)])
             pown[rows_of(s), pcols(p)] += rrem[0, :, pcols(p)]
-            rc(pown.at[rows_of(s), pcols(p)], rrem.at[2, :, pcols(p)], sr.at[l, p, 2], rr.at[l, p, 2], to(hop(s))).start()
+            rc(pown.at[rows_of(s), pcols(p)], rrem.at[2, :, pcols(p)], sr, rr.at[p, 2], to(hop(s))).start()
 
     def down_end(l, out):
         at = pl.ds(al((k * chips + c) * seq, seq), seq)
         for p in range(TILES):
             for j in (1, 2):
-                taken(rr.at[l, p, j], rrem.at[j, :, pcols(p)])
+                taken(rr.at[p, j], rrem.at[j, :, pcols(p)])
             acc = pown[rows_of(0), pcols(p)] + rrem[1, :, pcols(p)] + rrem[2, :, pcols(p)]
             out(pcols(p), (x1f[at, pcols(p)].astype(F32) + acc).astype(BF16))
 
     def down_sent(l):
-        for t in range(4):
-            taken(ss.at[l, t], psib.at[:, pl.ds(t * dtile, dtile)])
-        for p in range(TILES):
-            for j in range(3):
-                taken(sr.at[l, p, j], rrem.at[j, :, pcols(p)])
+        taken(ss, psib)
+        taken(sr, rrem)
 
     gains[...] = jnp.zeros_like(gains)
     mycols = pl.ds(al(f * blk, 128), blk)
@@ -300,128 +312,189 @@
     pl.semaphore_signal(barrier, inc=1, device_id=(partner, f), device_id_type=MESH)
     pl.semaphore_wait(barrier, n)
 
-    issue(0, WO, ALL)
-    issue(0, G0, ALL)
+    def load_down(l):
+        pltpu.make_async_copy(wd.at[l], wd_v.at[l], lsem.at[l, 7]).start()
+
+    def send_gains():
+        for i in range(1, n):
+            rc(gblock, gblock, sg, rg, to(i)).start()
+
+    def local_ready():
+        local_x.wait()
+        local_tab.wait()
+        taken(rg, gains.at[:, pl.ds(0, (n - 1) * blk)])
+
+    def own_all(l, groups):
+        for g in groups:
+            own(l, g)
+        load_down(l)
+
+    def down_ready(l):
+        taken(lsem.at[l, 7], wd_v.at[l])
+
+    def keep(cols, v):
+        xf[pl.ds(al((k * chips + c) * seq, seq), seq), cols] = v
+
+    def emit(cols, v):
+        yv[:, cols] = v
+        pltpu.make_async_copy(yv.at[:, cols], y_hbm.at[:, cols], lsem.at[1, 7]).start()
+
+    issue(0, WO, SAME)
+    issue(0, WO, CROSS)
+    issue(0, WO, FAR)
+    issue(0, WO, OTHER)
+    issue(0, G0, SAME)
+    issue(0, G0, CROSS)
+    issue(0, G0, FAR)
+    issue(0, G0, OTHER)
     gather_start(0, AX, x_hbm)
-    for i in range(1, n):
-        rc(gblock, gblock, sg.at[i], rg.at[i], to(i)).start()
-    issue(0, QKV, ALL)
-    for g in (WO, G0, G1, U0, U1):
-        own(0, g)
-    own_d = [pltpu.make_async_copy(wd.at[l], wd_v.at[l], lsem.at[l, 7]) for l in range(layers)]
-    own_d[0].start()
-    forward(0, WO)
-    forward(0, G0)
-
-    for l in range(layers):
-        last = l + 1 == layers
-        gather_near(l, AX)
-        if l == 0:
-            issue(l, G1, ALL)
-            forward(l, QKV)
-            gather_far(l, AX)
-            local_x.wait()
-            local_tab.wait()
-            for i in range(1, n):
-                taken(rg.at[i], gains.at[:, pl.ds(al(source(i) * blk, 128), blk)])
-        else:
-            issue(l, G0, CROSS)
-            issue(l, G1, FAR)
-            issue(l, G1, NEAR)
-            gather_far(l, AX)
-            forward(l, G0, NEAR)
-        gather_end(l, AX)
-        norm(xf, l)
-        if l == 0:
-            issue(l, U0, ALL)
-            forward(l, G1)
-        complete(l, QKV)
-        project(l)
-        attend(0, n // 2)
-        if l > 0:
-            forward(l, G1, FAR)
-        attend(n // 2, n)
-        gather_start(l, AO)
-        if l == 0:
-            issue(l, U1, SAME)
-            forward(l, U0)
-            gather_near(l, AO)
-            issue(l, U1, CROSS)
-            issue(l, U1, FAR)
-            forward(l, U1, SAME)
-            gather_far(l, AO)
-            forward(l, U1, CROSS)
-        else:
-            issue(l, U0, SAME)
-            forward(l, G1, NEAR)
-            gather_near(l, AO)
-            issue(l, U0, CROSS)
-            issue(l, U0, FAR)
-            issue(l, U1, FAR)
-            forward(l, U0, SAME)
-            gather_far(l, AO)
-            forward(l, U0, CROSS)
-        gather_end(l, AO)
-        complete(l, WO)
-        output_projection(l)
-        gather_start(l, AM)
-        if l == 0:
-            forward(l, U1, FAR)
-            gather_near(l, AM)
-            for part_of in (NEAR, FAR):
-                issue(l + 1, QKV, part_of)
-                issue(l + 1, WO, part_of)
-            for g in range(GROUPS):
-                own(l + 1, g)
-            own_d[l + 1].start()
-            gather_far(l, AM)
-        else:
-            issue(l, U1, SAME)
-            forward(l, U0, FAR)
-            forward(l, U1, FAR)
-            gather_near(l, AM)
-            issue(l, U1, CROSS)
-            forward(l, U1, SAME)
-            gather_far(l, AM)
-            forward(l, U1, CROSS)
-        gather_end(l, AM)
-        norm(x1f, layers + l)
-        complete(l, G0)
-        complete(l, U0)
-        gate_up(l, 0)
-        complete(l, G1)
-        complete(l, U1)
-        gate_up(l, 1)
-        own_d[l].wait()
-        down_start(l)
-        if not last:
-            def store(cols, v):
-                xf[pl.ds(al((k * chips + c) * seq, seq), seq), cols] = v
-
-            forward(l + 1, QKV)
-            forward(l + 1, WO)
-            down_pass(l)
-            issue(l + 1, G0, FAR)
-            down_end(l, store)
-            down_sent(l)
-            gather_start(l + 1, AX)
-            issue(l + 1, G0, SAME)
-            forward(l + 1, G0, FAR)
-        else:
-            def store(cols, v):
-                y_ref[:, cols] = v
-
-            down_pass(l)
-            down_end(l, store)
-            down_sent(l)
-
-    for i in range(1, n):
-        taken(sg.at[i], gblock)
+    send_gains()
+    issue(0, QKV, SAME)
+    issue(0, QKV, CROSS)
+    issue(0, QKV, FAR)
+    issue(0, QKV, OTHER)
+    own_all(0, (WO, G0, G1, U0, U1))
+    forward(0, WO, SAME)
+    forward(0, WO, CROSS)
+    forward(0, WO, FAR)
+    forward(0, G0, SAME)
+    forward(0, G0, CROSS)
+    forward(0, G0, FAR)
+    gather_near(0, AX)
+    issue(0, G1, SAME)
+    issue(0, G1, CROSS)
+    issue(0, G1, FAR)
+    issue(0, G1, OTHER)
+    forward(0, QKV, SAME)
+    forward(0, QKV, CROSS)
+    forward(0, QKV, FAR)
+    gather_far(0, AX)
+    local_ready()
+    gather_end(0, AX)
+    norm(xf, 0)
+    issue(0, U0, SAME)
+    issue(0, U0, CROSS)
+    issue(0, U0, FAR)
+    issue(0, U0, OTHER)
+    forward(0, G1, SAME)
+    forward(0, G1, CROSS)
+    forward(0, G1, FAR)
+    complete(0, QKV)
+    project(0)
+    attend(0, n // 2)
+    attend(n // 2, n)
+    gather_start(0, AO)
+    issue(0, U1, SAME)
+    forward(0, U0, SAME)
+    forward(0, U0, CROSS)
+    forward(0, U0, FAR)
+    gather_near(0, AO)
+    issue(0, U1, CROSS)
+    issue(0, U1, FAR)
+    issue(0, U1, OTHER)
+    forward(0, U1, SAME)
+    gather_far(0, AO)
+    gather_end(0, AO)
+    complete(0, WO)
+    output_projection(0)
+    gather_start(0, AM)
+    forward(0, U1, CROSS)
+    forward(0, U1, FAR)
+    gather_near(0, AM)
+    issue(1, QKV, SAME)
+    issue(1, QKV, CROSS)
+    issue(1, WO, SAME)
+    issue(1, WO, CROSS)
+    issue(1, QKV, FAR)
+    issue(1, QKV, OTHER)
+    issue(1, WO, FAR)
+    issue(1, WO, OTHER)
+    own_all(1, range(GROUPS))
+    gather_far(0, AM)
+    gather_end(0, AM)
+    norm(x1f, layers + 0)
+    complete(0, G0)
+    complete(0, U0)
+    gate_up(0, 0)
+    complete(0, G1)
+    complete(0, U1)
+    gate_up(0, 1)
+    down_ready(0)
+    down_start(0)
+    forward(1, QKV, SAME)
+    forward(1, QKV, CROSS)
+    forward(1, QKV, FAR)
+    forward(1, WO, SAME)
+    forward(1, WO, CROSS)
+    forward(1, WO, FAR)
+    down_pass(0)
+    issue(1, G0, SAME)
+    issue(1, G0, CROSS)
+    down_end(0, keep)
+    down_sent(0)
+    gather_start(1, AX)
+    issue(1, U0, SAME)
+    forward(1, G0, SAME)
+    forward(1, G0, CROSS)
+    gather_near(1, AX)
+    issue(1, U0, CROSS)
+    issue(1, G0, FAR)
+    issue(1, G0, OTHER)
+    issue(1, G1, SAME)
+    issue(1, G1, CROSS)
+    gather_far(1, AX)
+    issue(1, G1, FAR)
+    issue(1, G1, OTHER)
+    forward(1, U0, SAME)
+    gather_end(1, AX)
+    norm(xf, 1)
+    complete(1, QKV)
+    project(1)
+    forward(1, U0, CROSS)
+    attend(0, n // 2)
+    forward(1, G0, FAR)
+    attend(n // 2, n)
+    gather_start(1, AO)
+    issue(1, U1, SAME)
+    forward(1, G1, SAME)
+    forward(1, G1, CROSS)
+    gather_near(1, AO)
+    issue(1, U1, CROSS)
+    forward(1, G1, FAR)
+    forward(1, U1, SAME)
+    gather_far(1, AO)
+    issue(1, U0, FAR)
+    issue(1, U0, OTHER)
+    issue(1, U1, FAR)
+    issue(1, U1, OTHER)
+    gather_end(1, AO)
+    complete(1, WO)
+    output_projection(1)
+    gather_start(1, AM)
+    forward(1, U1, CROSS)
+    forward(1, U0, FAR)
+    forward(1, U1, FAR)
+    gather_near(1, AM)
+    gather_far(1, AM)
+    gather_end(1, AM)
+    norm(x1f, layers + 1)
+    complete(1, G0)
+    complete(1, U0)
+    gate_up(1, 0)
+    complete(1, G1)
+    complete(1, U1)
+    gate_up(1, 1)
+    down_ready(1)
+    down_start(1)
+    down_pass(1)
+    down_end(1, emit)
+    down_sent(1)
+    taken(lsem.at[1, 7], yv)
+    taken(sg, gains.at[:, pl.ds(0, (n - 1) * blk)])
     for l in range(layers):
         for g in range(GROUPS):
-            taken(sw.at[l, g], bytes_of(l, g, len(REMOTE) * TAKE[l][g] + blk))
-            if TAKE[l][g] < blk:
-                taken(sf.at[l, g], bytes_of(l, g, len(REMOTE) * (blk - TAKE[l][g])))
+            taken(sw.at[l, g], bytes_of(l, g, n * blk - blk - brought(l, g)))
+            taken(sf.at[l, g], bytes_of(l, g, brought(l, g)))
 
 
 def rope_tables(seq, hd):
@@ -458,7 +531,7 @@
             functools.partial(kernel, n),
             out_shape=jax.ShapeDtypeStruct((seq, width), BF16),
             in_specs=[anyspace, vmem, vmem] + [anyspace] * 8,
-            out_specs=vmem,
+                out_specs=anyspace,
             scratch_shapes=[
                 pltpu.VMEM((tokens, width), BF16),
                 pltpu.VMEM((tokens, width), BF16),
@@ -473,16 +546,17 @@
                 pltpu.VMEM((layers, width, ffn), BF16),
                 pltpu.VMEM((layers, width, ffn), BF16),
                 pltpu.VMEM((layers, ffn, width), BF16),
+                pltpu.VMEM((seq, width), BF16),
                 pltpu.VMEM((half, width), F32),
                 pltpu.VMEM((half, width), F32),
                 pltpu.VMEM((half, width), F32),
                 pltpu.VMEM((3, seq, width), F32),
-                dma((layers, GROUPS)), dma((layers, GROUPS, n)),
+                dma((layers, GROUPS)), dma((layers, GROUPS, 4)),
                 dma((layers, GROUPS)), dma((layers, GROUPS)),
-                dma((layers, 3, n)), dma((layers, 3, n)),
-                dma((n,)), dma((n,)),
-                dma((layers, 4)), dma((layers, 4)),
-                dma((layers, TILES, 3)), dma((layers, TILES, 3)),
+                dma((3,)), dma((3, n)),
+                dma, dma,
+                dma, dma((STEPS,)),
+                dma, dma((TILES, 3)),
                 dma((layers, 8)),
             ],
             compiler_params=pltpu.CompilerParams(collective_id=0, has_side_effects=True, vmem_limit_bytes=63 * 2**20),

time: 238 us -> 234 us (0.983)
  Pallas kernels: 237 us -> 232 us
    pallas_call x1, Pallas kernels: 237 us -> 232 us  [local_forward(): pl.pallas_call(functools.partial(kernel, n), out_shape=jax.ShapeDtypeStru...]
where the time goes in v3:
time: 234 us
  Pallas kernels  232 us (99%)
    pallas_call x1, Pallas kernels, local_forward(): pl.pallas_call(functools.partial(kernel, n), out_shape=jax.ShapeDtypeStru...  232 us

profile of v3, /device:TPU:113, one launch (start us, length us, event | category | flops | bytes accessed | tf_op | source)
XLA Modules:
  0.0 233.5 jit_solution(6977533694148985854)
XLA Ops:
  0.0 231.9 %shard_map.109 = bf16[64,2048]{1,0:T(8,128)(2,1)} custom-call(bf16[64,2048]{1,0:T(8,128)(2,1)} %bitcast.15, bf16[2,256]{1,0:T(2,128)(2,1)} %an_ref.1, bf16[2,256]{1,0:T(2,128)(2,1)} %mn_ref.1, f32[2,64,128]{2,1,0:T(8,128)} %constant.2.clone.tab_hbm, bf16[2,2048,256]{2,1,0:T(8,128)(2,1)} %bitcast.11, bf16[2,512,256]{2,1,0:T(8,128)(2,1)} %bitcast.13, ...), custom_call_target="tpu_custom_call" | custom-call | tf_op jit(solution)/shard_map/pallas_call | solution.py:530
  231.9 1.7 copy.13
